TPU v7x, 32 devices: a whole 2x2x4 slice. The times are simulated.
32 devices in a mesh: ctx: 16 (over z, y, x), head: 2 (over core).
Axes of the slice: x: 2, y: 2, z: 4, core: 2. Of those that a mesh axis runs over, the one named last changes fastest.
Arguments:
- query: bfloat16 [2048, 384], P('ctx', 'head'), may hold values from -48 to 48
- key_nope: bfloat16 [2048, 256], P('ctx', 'head'), may hold values from -8 to 8
- key_rope: bfloat16 [2048, 64], P('ctx'), may hold values from -8 to 8
- value: bfloat16 [2048, 256], P('ctx', 'head'), may hold values from -6 to 6
- d_out: bfloat16 [2048, 256], P('ctx', 'head'), may hold values from -288 to 288
- positions: int32 [2048], P('ctx'), may hold values from 0 to 2047, as said below
- segments: int32 [2048], replicated, may hold values from 0 to 3, never falling along the last dimension, each value on 1 to 1024 neighbouring positions
Outputs:
- d_query: bfloat16 [2048, 384], P('ctx', 'head')
- d_key_nope: bfloat16 [2048, 256], P('ctx', 'head')
- d_key_rope: bfloat16 [2048, 64], P('ctx')
- d_value: bfloat16 [2048, 256], P('ctx', 'head')
Inputs may be any that keep to these rules, and one draw needn't show every extreme that they name: A permutation of 0 to 2047 made of aligned blocks of 32 rows holding 32 consecutive positions in order.
All inputs are finite; a program needn't handle non-finite values.
Results may differ from a plain program's by a relative error of at most 0.0049.
Values may be sent and summed in bfloat16 or wider, within the bound.
A program may use at most 64 MiB of HBM per device.

v0:
```python
import math
import jax
import jax.numpy as jnp
from jax import lax
from jax.sharding import PartitionSpec as P

NOPE = 128
ROPE = 64
VD = 128
QK = 192
clip_ratio = 0.25
block_limit = 1024


def split_heads(array, width):
    return array.reshape(array.shape[0], -1, width)


def make_keys(nope_rows, rope_rows):
    nope_three = split_heads(nope_rows, NOPE)
    rope_three = rope_rows[:, None, :]
    return jnp.concatenate([nope_three, rope_three], axis=2)


def visible(query_place, query_doc, key_place, key_doc):
    return (query_doc[:, None] == key_doc[None, :]) & (key_place[None, :] <= query_place[:, None])


def over_blocks(advance, carried, pieces, offset=0):
    row_count = pieces[0].shape[0]
    blocks = row_count // block_limit
    parts = jax.tree.map(
        lambda array: array.reshape((blocks, block_limit) + array.shape[1:]), pieces
    )

    def visitor(state_now, part_now):
        return (advance(state_now, part_now, offset), None)

    carried, unused = lax.scan(visitor, carried, parts)
    return carried


def shards(query, key_nope, key_rope, value, d_out, positions, segments):
    softmax_scale = 1.0 / math.sqrt(QK)
    documents = jnp.take(segments, positions)
    local_rows = query.shape[0]
    heads_here = query.shape[1] // QK
    query_three = split_heads(query, QK)
    dout_three = split_heads(d_out, VD)

    def soft_advance(carried, pieces, offset):
        row_max, row_sum, weighted = carried
        piece_nope, piece_rope, piece_value, piece_place, piece_doc = pieces
        key_rows = make_keys(piece_nope, piece_rope)
        scores = (
            jnp.einsum("qhd,khd->hqk", query_three, key_rows, preferred_element_type=jnp.float32)
            * softmax_scale
        )
        allowed = visible(positions, documents, piece_place, piece_doc)[None]
        scores = jnp.where(allowed, scores, -jnp.inf)
        new_max = jnp.maximum(row_max, jnp.max(scores, axis=2))
        safe_max = jnp.where(new_max == -jnp.inf, 0.0, new_max)
        exponent = jnp.exp(scores - safe_max[:, :, None])
        d_prob = jnp.einsum(
            "qhv,khv->hqk",
            dout_three,
            split_heads(piece_value, VD),
            preferred_element_type=jnp.float32,
        )
        shrink = jnp.exp(row_max - safe_max)
        return (
            new_max,
            row_sum * shrink + jnp.sum(exponent, axis=2),
            weighted * shrink + jnp.sum(exponent * d_prob, axis=2),
        )

    soft_init = (
        jnp.full((heads_here, local_rows), -jnp.inf, jnp.float32),
        jnp.zeros((heads_here, local_rows), jnp.float32),
        jnp.zeros((heads_here, local_rows), jnp.float32),
    )
    soft_state = over_blocks(
        soft_advance,
        soft_init,
        (
            lax.all_gather(key_nope, "ctx", axis=0, tiled=True),
            lax.all_gather(key_rope, "ctx", axis=0, tiled=True),
            lax.all_gather(value, "ctx", axis=0, tiled=True),
            lax.all_gather(positions, "ctx", axis=0, tiled=True),
            lax.all_gather(documents, "ctx", axis=0, tiled=True),
        ),
        jnp.int32(0),
    )
    row_max, row_sum, weighted = soft_state
    log_total = row_max + jnp.log(row_sum)
    row_delta = weighted / row_sum

    def query_advance(grad_query, pieces, offset):
        piece_nope, piece_rope, piece_value, piece_place, piece_doc = pieces
        key_rows = make_keys(piece_nope, piece_rope)
        scores = (
            jnp.einsum("qhd,khd->hqk", query_three, key_rows, preferred_element_type=jnp.float32)
            * softmax_scale
        )
        allowed = visible(positions, documents, piece_place, piece_doc)[None]
        weights = jnp.exp(jnp.where(allowed, scores, -jnp.inf) - log_total[:, :, None])
        d_prob = jnp.einsum(
            "qhv,khv->hqk",
            dout_three,
            split_heads(piece_value, VD),
            preferred_element_type=jnp.float32,
        )
        d_score = (weights * (d_prob - row_delta[:, :, None])).astype(jnp.bfloat16)
        return (
            grad_query
            + jnp.einsum("hqk,khd->qhd", d_score, key_rows, preferred_element_type=jnp.float32)
            * softmax_scale
        )

    query_init = jnp.zeros((local_rows, heads_here, QK), jnp.float32)
    grad_query = over_blocks(
        query_advance,
        query_init,
        (
            lax.all_gather(key_nope, "ctx", axis=0, tiled=True),
            lax.all_gather(key_rope, "ctx", axis=0, tiled=True),
            lax.all_gather(value, "ctx", axis=0, tiled=True),
            lax.all_gather(positions, "ctx", axis=0, tiled=True),
            lax.all_gather(documents, "ctx", axis=0, tiled=True),
        ),
        jnp.int32(0),
    )
    local_keys = make_keys(key_nope, key_rope)
    value_three = split_heads(value, VD)

    def key_advance(carried, pieces, offset):
        grad_key, grad_value = carried
        piece_query, piece_dout, piece_log, piece_delta, piece_place, piece_doc = pieces
        piece_query_three = split_heads(piece_query, QK)
        piece_dout_three = split_heads(piece_dout, VD)
        scores = (
            jnp.einsum(
                "qhd,khd->hqk", piece_query_three, local_keys, preferred_element_type=jnp.float32
            )
            * softmax_scale
        )
        allowed = visible(piece_place, piece_doc, positions, documents)[None]
        weights = jnp.exp(jnp.where(allowed, scores, -jnp.inf) - piece_log.T[:, :, None])
        d_prob = jnp.einsum(
            "qhv,khv->hqk", piece_dout_three, value_three, preferred_element_type=jnp.float32
        )
        d_score = (weights * (d_prob - piece_delta.T[:, :, None])).astype(jnp.bfloat16)
        grad_key = (
            grad_key
            + jnp.einsum(
                "hqk,qhd->khd", d_score, piece_query_three, preferred_element_type=jnp.float32
            )
            * softmax_scale
        )
        grad_value = grad_value + jnp.einsum(
            "hqk,qhv->khv",
            weights.astype(jnp.bfloat16),
            piece_dout_three,
            preferred_element_type=jnp.float32,
        )
        return (grad_key, grad_value)

    key_init = (
        jnp.zeros((local_rows, heads_here, QK), jnp.float32),
        jnp.zeros((local_rows, heads_here, VD), jnp.float32),
    )
    grad_key, grad_value = over_blocks(
        key_advance,
        key_init,
        (
            lax.all_gather(query.astype(jnp.float32), "ctx", axis=0, tiled=True).astype(
                jnp.bfloat16
            ),
            lax.all_gather(d_out.astype(jnp.float32), "ctx", axis=0, tiled=True).astype(
                jnp.bfloat16
            ),
            lax.all_gather(log_total.T, "ctx", axis=0, tiled=True),
            lax.all_gather(row_delta.T, "ctx", axis=0, tiled=True),
            lax.all_gather(positions, "ctx", axis=0, tiled=True),
            lax.all_gather(documents, "ctx", axis=0, tiled=True),
        ),
        jnp.int32(0),
    )
    grad_nope = grad_key[:, :, :NOPE]
    rope_part = jnp.sum(grad_key[:, :, NOPE:], axis=1)
    local_squares = (
        jnp.sum(jnp.square(grad_query))
        + jnp.sum(jnp.square(grad_nope))
        + jnp.sum(jnp.square(grad_value))
    )
    rope_summed = lax.psum(rope_part, "head")
    first_head = (lax.axis_index("head") == 0).astype(jnp.float32)
    local_squares = local_squares + first_head * jnp.sum(jnp.square(rope_summed))
    total = lax.psum(local_squares, ("ctx", "head"))
    count_all = float(
        local_rows
        * lax.axis_size("ctx")
        * (heads_here * lax.axis_size("head") * (QK + NOPE + VD) + ROPE)
    )
    factor = jnp.minimum(1.0, clip_ratio * math.sqrt(count_all) / jnp.sqrt(total))
    d_key_rope = (rope_summed * factor).astype(jnp.bfloat16)
    d_query = (grad_query * factor).astype(jnp.bfloat16).reshape(local_rows, heads_here * QK)
    d_key_nope = (grad_nope * factor).astype(jnp.bfloat16).reshape(local_rows, heads_here * NOPE)
    d_value = (grad_value * factor).astype(jnp.bfloat16).reshape(local_rows, heads_here * VD)
    return (d_query, d_key_nope, d_key_rope, d_value)


def solution(mesh):
    return jax.shard_map(
        shards,
        mesh=mesh,
        in_specs=(
            P("ctx", "head"),
            P("ctx", "head"),
            P("ctx", None),
            P("ctx", "head"),
            P("ctx", "head"),
            P("ctx"),
            P(),
        ),
        out_specs=(P("ctx", "head"), P("ctx", "head"), P("ctx", None), P("ctx", "head")),
        check_vma=False,
    )
```

profile of v0, /device:TPU:12, one launch (start us, length us, event | category | flops | bytes accessed | tf_op | source)
XLA Modules:
  0.0 411.8 jit_solution(17462087313874825854)
XLA Ops:
  0.7 34.1 %all_gather.34 = bf16[2048,128]{1,0:T(8,128)(2,1)S(1)} all-gather(bf16[128,128]{1,0:T(8,128)(2,1)} %param.14), channel_id=1, replica_groups=mesh['ctx'=16,'head'=2] {'ctx'}, dimensions={0}, use_global_device_ids=true | all-gather | bytes 557056 | tf_op jit(solution)/shard_map/all_gather | solution.py:125
  34.7 37.1 %all_gather.35 = bf16[2048,64]{0,1:T(8,128)(2,1)S(1)} all-gather(bf16[128,64]{0,1:T(8,128)(2,1)S(1)} %copy-done.4), channel_id=1, replica_groups=mesh['ctx'=16,'head'=2] {'ctx'}, dimensions={0}, use_global_device_ids=true | all-gather | bytes 278528 | tf_op jit(solution)/shard_map/all_gather | solution.py:126
  72.2 0.6 copy-done.6
  72.8 1.1 gather_fusion
  74.0 37.4 %all-gather.2 = s32[16,1,128]{2,1,0:T(1,128)S(1)} all-gather(s32[1,1,128]{2,1,0:T(1,128)S(1)} %bitcast.246), channel_id=1, replica_groups=mesh['ctx'=16,'head'=2] {'ctx'}, dimensions={0}, use_global_device_ids=true | all-gather | bytes 8704 | tf_op jit(solution)/shard_map/all_gather | solution.py:129
  111.4 0.5 broadcast.162
  111.9 0.7 reduce.12
  112.6 35.7 %all-gather.3 = s32[16,1,128]{2,1,0:T(1,128)S(1)} all-gather(s32[1,1,128]{2,1,0:T(1,128)S(1)} %bitcast.245), channel_id=1, replica_groups=mesh['ctx'=16,'head'=2] {'ctx'}, dimensions={0}, use_global_device_ids=true | all-gather | bytes 8704 | tf_op jit(solution)/shard_map/all_gather | solution.py:128
  148.2 0.7 reduce.13
  149.0 40.6 %all_gather.38 = bf16[2048,128]{1,0:T(8,128)(2,1)S(1)} all-gather(bf16[128,128]{1,0:T(8,128)(2,1)S(1)} %copy-done.2), channel_id=1, replica_groups=mesh['ctx'=16,'head'=2] {'ctx'}, dimensions={0}, use_global_device_ids=true | all-gather | bytes 557056 | tf_op jit(solution)/shard_map/all_gather | solution.py:127
  189.6 2.0 while.39
  191.6 2.0 while.40
  191.9 0.7 fusion.120
  192.9 0.7 fusion.120
  193.6 0.6 multiply_reduce_fusion
  194.3 40.7 %all_gather.39 = bf16[2048,192]{0,1:T(8,128)(2,1)S(1)} all-gather(bf16[128,192]{0,1:T(8,128)(2,1)S(1)} %bitcast.242), channel_id=1, replica_groups=mesh['ctx'=16,'head'=2] {'ctx'}, dimensions={0}, use_global_device_ids=true | all-gather | bytes 835584 | tf_op jit(solution)/shard_map/all_gather | solution.py:176
  234.9 0.5 copy.24
  235.6 0.6 copy-done.3
  236.3 37.2 %all-gather = f32[1,2048]{1,0:T(1,128)S(1)} all-gather(f32[1,128]{1,0:T(1,128)S(1)} %get-tuple-element.874), channel_id=2, replica_groups=mesh['ctx'=16,'head'=2] {'ctx'}, dimensions={1}, use_global_device_ids=true | all-gather | bytes 8704 | tf_op jit(solution)/shard_map/all_gather | solution.py:182
  273.5 38.5 %all_gather.41 = bf16[2048,128]{1,0:T(8,128)(2,1)S(1)} all-gather(bf16[128,128]{1,0:T(8,128)(2,1)S(1)} %bitcast.227), channel_id=1, replica_groups=mesh['ctx'=16,'head'=2] {'ctx'}, dimensions={0}, use_global_device_ids=true | all-gather | bytes 557056 | tf_op jit(solution)/shard_map/all_gather | solution.py:179
  312.0 37.3 %all-gather.1 = f32[1,2048]{1,0:T(1,128)S(1)} all-gather(f32[1,128]{1,0:T(1,128)S(1)} %get-tuple-element.873), channel_id=3, replica_groups=mesh['ctx'=16,'head'=2] {'ctx'}, dimensions={1}, use_global_device_ids=true | all-gather | bytes 8704 | tf_op jit(solution)/shard_map/all_gather | solution.py:183
  349.2 2.7 while.41
  349.8 0.5 fusion.129
  351.1 0.5 fusion.129
  352.1 0.6 multiply_reduce_fusion.2
  354.0 0.6 multiply_reduce_fusion.1
  355.3 3.4 psum.14
  358.7 0.6 multiply_reduce_fusion.3
  360.0 49.1 %psum.15 = f32[]{:T(128)} all-reduce(f32[]{:T(128)S(6)} %add.53), channel_id=1, replica_groups=mesh['ctx'=16,'head'=2] {'ctx','head'}, use_global_device_ids=true, to_apply=%region_14.15 | all-reduce | flops 1 | bytes 8 | tf_op jit(solution)/shard_map/psum | solution.py:199
  409.8 0.6 fusion.82
  410.5 0.6 fusion.83
  411.1 0.6 multiply_convert_fusion.3
  (65 shorter events, 4.8 us)
Async XLA Ops:
  0.6 72.2 %copy-start = (s32[2048]{0:T(1024)S(1)}, s32[2048]{0:T(1024)}, u32[]{:S(2)}) copy-start(s32[2048]{0:T(1024)} %param.19) | copy-start | bytes 24580
  0.7 34.1 %copy-start.4 = (bf16[128,64]{0,1:T(8,128)(2,1)S(1)}, bf16[128,64]{0,1:T(8,128)(2,1)}, u32[]{:S(2)}) copy-start(bf16[128,64]{0,1:T(8,128)(2,1)} %param.15) | copy-start | bytes 49156
  72.2 0.7 copy-start.6
  112.5 36.4 %copy-start.2 = (bf16[128,128]{1,0:T(8,128)(2,1)S(1)}, bf16[128,128]{1,0:T(8,128)(2,1)}, u32[]{:S(2)}) copy-start(bf16[128,128]{1,0:T(8,128)(2,1)} %param.16) | copy-start | bytes 98308
  149.0 40.6 %copy-start.1 = (bf16[128,128]{1,0:T(8,128)(2,1)S(1)}, bf16[128,128]{1,0:T(8,128)(2,1)}, u32[]{:S(2)}) copy-start(bf16[128,128]{1,0:T(8,128)(2,1)} %param.17) | copy-start | bytes 98308
  149.0 40.6 %copy-start.5 = (bf16[128,192]{0,1:T(8,128)(2,1)S(1)}, bf16[128,192]{0,1:T(8,128)(2,1)}, u32[]{:S(2)}) copy-start(bf16[128,192]{0,1:T(8,128)(2,1)} %param.13) | copy-start | bytes 147460
  235.4 0.8 copy-start.3
where the time goes:
time: 412 us
  blocking collectives  391 us (95%)
  other arithmetic  6.09 us (1%)
  matrix products  5.79 us (1%)
  local copies, waits for them, and re-layouts  4.48 us (1%)
  between operations  4.17 us (1%)
    psum x1, blocking collectives, shards(): total = lax.psum(local_squares, ('ctx', 'head'))  49.1 us
    all_gather x1, blocking collectives, shards(): lax.all_gather(query.astype(jnp.float32), 'ctx', axis=0, tiled=True)  40.7 us
    all_gather x1, blocking collectives, shards(): lax.all_gather(value, 'ctx', axis=0, tiled=True)  40.6 us
    all_gather x1, blocking collectives, shards(): lax.all_gather(d_out.astype(jnp.float32), 'ctx', axis=0, tiled=True)  38.5 us
    all_gather x1, blocking collectives, shards(): lax.all_gather(documents, 'ctx', axis=0, tiled=True)  37.4 us
    all_gather x1, blocking collectives, shards(): lax.all_gather(row_delta.T, 'ctx', axis=0, tiled=True)  37.3 us
    all_gather x1, blocking collectives, shards(): lax.all_gather(log_total.T, 'ctx', axis=0, tiled=True)  37.2 us
    all_gather x1, blocking collectives, shards(): lax.all_gather(key_rope, 'ctx', axis=0, tiled=True)  37.1 us

commit v1 on v0

--- a/solution.py
+++ b/solution.py
@@ -196,7 +196,7 @@
     rope_summed = lax.psum(rope_part, "head")
     first_head = (lax.axis_index("head") == 0).astype(jnp.float32)
     local_squares = local_squares + first_head * jnp.sum(jnp.square(rope_summed))
-    total = lax.psum(local_squares, ("ctx", "head"))
+    total = jnp.sum(lax.all_gather(local_squares, ("ctx", "head")), axis=0)
     count_all = float(
         local_rows
         * lax.axis_size("ctx")

time: 412 us -> 413 us (level)
    psum x1 -> x0, blocking collectives: 49.1 us -> none  [shards(): total = lax.psum(local_squares, ('ctx', 'head'))]
    unnamed x0 -> x1, blocking collectives: none -> 48.9 us
where the time goes in v1:
time: 413 us; the launch traced here: 412 us
  blocking collectives  391 us (95%)
  other arithmetic  6.69 us (2%)
  matrix products  5.79 us (1%)
  local copies, waits for them, and re-layouts  4.6 us (1%)
  between operations  4.18 us (1%)
    unnamed x1, blocking collectives  48.9 us
    all_gather x1, blocking collectives, shards(): lax.all_gather(query.astype(jnp.float32), 'ctx', axis=0, tiled=True)  40.7 us
    all_gather x1, blocking collectives, shards(): lax.all_gather(value, 'ctx', axis=0, tiled=True)  40.6 us
    all_gather x1, blocking collectives, shards(): lax.all_gather(d_out.astype(jnp.float32), 'ctx', axis=0, tiled=True)  38.5 us
    all_gather x1, blocking collectives, shards(): lax.all_gather(documents, 'ctx', axis=0, tiled=True)  37.4 us
    all_gather x1, blocking collectives, shards(): lax.all_gather(row_delta.T, 'ctx', axis=0, tiled=True)  37.3 us
    all_gather x1, blocking collectives, shards(): lax.all_gather(log_total.T, 'ctx', axis=0, tiled=True)  37.2 us
    all_gather x1, blocking collectives, shards(): lax.all_gather(key_rope, 'ctx', axis=0, tiled=True)  37.1 us

profile of v1, /device:TPU:12, one launch (start us, length us, event | category | flops | bytes accessed | tf_op | source)
XLA Modules:
  0.0 412.2 jit_solution(13939883977414014317)
XLA Ops:
  0.7 34.1 %all_gather.40 = bf16[2048,128]{1,0:T(8,128)(2,1)S(1)} all-gather(bf16[128,128]{1,0:T(8,128)(2,1)} %param.14), channel_id=1, replica_groups=mesh['ctx'=16,'head'=2] {'ctx'}, dimensions={0}, use_global_device_ids=true | all-gather | bytes 557056 | tf_op jit(solution)/shard_map/all_gather | solution.py:125
  34.7 37.1 %all_gather.41 = bf16[2048,64]{0,1:T(8,128)(2,1)S(1)} all-gather(bf16[128,64]{0,1:T(8,128)(2,1)S(1)} %copy-done.4), channel_id=1, replica_groups=mesh['ctx'=16,'head'=2] {'ctx'}, dimensions={0}, use_global_device_ids=true | all-gather | bytes 278528 | tf_op jit(solution)/shard_map/all_gather | solution.py:126
  72.2 0.6 copy-done.6
  72.8 1.1 gather_fusion
  74.0 37.4 %all-gather.2 = s32[16,1,128]{2,1,0:T(1,128)S(1)} all-gather(s32[1,1,128]{2,1,0:T(1,128)S(1)} %bitcast.247), channel_id=1, replica_groups=mesh['ctx'=16,'head'=2] {'ctx'}, dimensions={0}, use_global_device_ids=true | all-gather | bytes 8704 | tf_op jit(solution)/shard_map/all_gather | solution.py:129
  111.4 0.5 broadcast.163
  111.9 0.7 reduce.13
  112.6 35.7 %all-gather.3 = s32[16,1,128]{2,1,0:T(1,128)S(1)} all-gather(s32[1,1,128]{2,1,0:T(1,128)S(1)} %bitcast.246), channel_id=1, replica_groups=mesh['ctx'=16,'head'=2] {'ctx'}, dimensions={0}, use_global_device_ids=true | all-gather | bytes 8704 | tf_op jit(solution)/shard_map/all_gather | solution.py:128
  148.2 0.7 reduce.14
  149.0 40.6 %all_gather.44 = bf16[2048,128]{1,0:T(8,128)(2,1)S(1)} all-gather(bf16[128,128]{1,0:T(8,128)(2,1)S(1)} %copy-done.2), channel_id=1, replica_groups=mesh['ctx'=16,'head'=2] {'ctx'}, dimensions={0}, use_global_device_ids=true | all-gather | bytes 557056 | tf_op jit(solution)/shard_map/all_gather | solution.py:127
  189.6 2.0 while.39
  191.6 2.0 while.40
  191.9 0.7 fusion.120
  192.9 0.7 fusion.120
  193.6 0.6 multiply_reduce_fusion
  194.3 40.7 %all_gather.45 = bf16[2048,192]{0,1:T(8,128)(2,1)S(1)} all-gather(bf16[128,192]{0,1:T(8,128)(2,1)S(1)} %bitcast.243), channel_id=1, replica_groups=mesh['ctx'=16,'head'=2] {'ctx'}, dimensions={0}, use_global_device_ids=true | all-gather | bytes 835584 | tf_op jit(solution)/shard_map/all_gather | solution.py:176
  235.6 0.6 copy-done.3
  236.3 37.2 %all-gather = f32[1,2048]{1,0:T(1,128)S(1)} all-gather(f32[1,128]{1,0:T(1,128)S(1)} %get-tuple-element.874), channel_id=2, replica_groups=mesh['ctx'=16,'head'=2] {'ctx'}, dimensions={1}, use_global_device_ids=true | all-gather | bytes 8704 | tf_op jit(solution)/shard_map/all_gather | solution.py:182
  273.5 38.5 %all_gather.47 = bf16[2048,128]{1,0:T(8,128)(2,1)S(1)} all-gather(bf16[128,128]{1,0:T(8,128)(2,1)S(1)} %bitcast.228), channel_id=1, replica_groups=mesh['ctx'=16,'head'=2] {'ctx'}, dimensions={0}, use_global_device_ids=true | all-gather | bytes 557056 | tf_op jit(solution)/shard_map/all_gather | solution.py:179
  312.0 37.3 %all-gather.1 = f32[1,2048]{1,0:T(1,128)S(1)} all-gather(f32[1,128]{1,0:T(1,128)S(1)} %get-tuple-element.873), channel_id=3, replica_groups=mesh['ctx'=16,'head'=2] {'ctx'}, dimensions={1}, use_global_device_ids=true | all-gather | bytes 8704 | tf_op jit(solution)/shard_map/all_gather | solution.py:183
  349.2 2.7 while.41
  349.8 0.5 fusion.129
  351.1 0.5 fusion.129
  352.1 0.6 multiply_reduce_fusion.2
  354.0 0.6 multiply_reduce_fusion.1
  355.3 3.4 psum.7
  358.7 0.6 multiply_reduce_fusion.3
  360.1 48.9 %all-reduce = f32[32]{0:T(128)S(1)} all-reduce(f32[32]{0:T(128)S(1)} %dynamic-update-slice), channel_id=1, replica_groups=mesh['ctx'=16,'head'=2] {'ctx','head'}, use_global_device_ids=true, to_apply=%add | all-reduce | flops 32 | bytes 256
  409.0 0.6 reduce_sum.78
  410.2 0.6 fusion.82
  411.0 0.6 fusion.83
  411.6 0.6 multiply_convert_fusion.3
  (68 shorter events, 5.5 us)
Async XLA Ops:
  0.6 72.2 %copy-start = (s32[2048]{0:T(1024)S(1)}, s32[2048]{0:T(1024)}, u32[]{:S(2)}) copy-start(s32[2048]{0:T(1024)} %param.19) | copy-start | bytes 24580
  0.7 34.1 %copy-start.4 = (bf16[128,64]{0,1:T(8,128)(2,1)S(1)}, bf16[128,64]{0,1:T(8,128)(2,1)}, u32[]{:S(2)}) copy-start(bf16[128,64]{0,1:T(8,128)(2,1)} %param.15) | copy-start | bytes 49156
  72.2 0.7 copy-start.6
  112.5 36.4 %copy-start.2 = (bf16[128,128]{1,0:T(8,128)(2,1)S(1)}, bf16[128,128]{1,0:T(8,128)(2,1)}, u32[]{:S(2)}) copy-start(bf16[128,128]{1,0:T(8,128)(2,1)} %param.16) | copy-start | bytes 98308
  149.0 40.6 %copy-start.1 = (bf16[128,128]{1,0:T(8,128)(2,1)S(1)}, bf16[128,128]{1,0:T(8,128)(2,1)}, u32[]{:S(2)}) copy-start(bf16[128,128]{1,0:T(8,128)(2,1)} %param.17) | copy-start | bytes 98308
  149.0 40.6 %copy-start.5 = (bf16[128,192]{0,1:T(8,128)(2,1)S(1)}, bf16[128,192]{0,1:T(8,128)(2,1)}, u32[]{:S(2)}) copy-start(bf16[128,192]{0,1:T(8,128)(2,1)} %param.13) | copy-start | bytes 147460
  235.4 0.8 copy-start.3
